TPU v7x, 128 devices: a whole 4x4x4 slice. The times are simulated.
128 devices in a mesh: gx: 2 (over z_lo), gy: 2 (over core), gz: 32 (over z_hi, y, x).
Axes of the slice: x: 4, y: 4, z: 4 (z_hi: 2, z_lo: 2; z = z_hi * 2 + z_lo), core: 2. Of those that a mesh axis runs over, the one named last changes fastest.
Arguments:
- state_re: float32 [134217728], P(('gx', 'gy', 'gz')), may hold values from -6 to 6
- state_im: float32 [134217728], P(('gx', 'gy', 'gz')), may hold values from -6 to 6
Outputs:
- out_re: float32 [134217728], P(('gx', 'gy', 'gz'))
- out_im: float32 [134217728], P(('gx', 'gy', 'gz'))
- probability: float32 [134217728], P(('gx', 'gy', 'gz'))
All inputs are finite; a program needn't handle non-finite values.
Results may differ from a plain program's by a relative error of at most 0.000071.
Values sent between devices are 32-bit elements; how exact they have to be, the bound alone decides.
A program may use at most 128 MiB of HBM per device.

v0:
```python
import functools

import jax
import jax.numpy as jnp
import numpy as np
from jax import lax
from jax.experimental import pallas as pl
from jax.experimental.pallas import tpu as pltpu
from jax.sharding import PartitionSpec as P

MESH = pl.DeviceIdType.MESH
AXES = ("gx", "gy", "gz")
N, B, C = 128, 64, 128
CHUNKS = 8
ROWS = B // CHUNKS
LOG_TOTAL = 27


def rev(values, bits):
    values = np.asarray(values)
    return sum(((values >> i) & 1) << (bits - 1 - i) for i in range(bits))


def wave(product, bits):
    angle = 2.0 * np.pi * (product % (1 << bits)) / (1 << bits)
    return np.cos(angle), np.sin(angle)


def split(matrix):
    high = jnp.asarray(matrix, jnp.float32).astype(jnp.bfloat16)
    low = (jnp.asarray(matrix, jnp.float32) - high.astype(jnp.float32)).astype(jnp.bfloat16)
    return high, low


def np_split(matrix):
    high = np.asarray(matrix, np.float32).astype(jnp.bfloat16)
    low = (np.asarray(matrix, np.float64) - high.astype(np.float64)).astype(jnp.bfloat16)
    return high, low


def tables():
    i = np.arange(N)
    k = rev(i, 7)
    wr, wi = wave(np.outer(k, i), 7)
    mix = np.block([[wr, -wi], [wi, wr]])
    both = lambda pair: np.concatenate(pair, axis=0).astype(np.float32)
    owner = both(wave(np.outer(k, i), 14))
    low_in = both(wave(np.outer(k, i), 27))
    low_out = both(wave(np.outer(k, i), 20))
    e = np.arange(8)
    steps = np.zeros((2 * N, C), np.float32)
    for at, bits in ((0, 20), (32, 13)):
        steps[:, at : at + 8] = both(wave(np.outer(k, e), bits))
        steps[:, at + 8 : at + 16] = both(wave(np.outer(k, 8 * e), bits))
    j = np.arange(B)
    kb = rev(j, 6)
    br, bi = wave(np.outer(kb, j), 6)
    b_hi, b_lo = np_split(np.block([[br, -bi], [bi, br]]))
    inner = np.concatenate([b_hi, b_hi, b_lo], axis=1)
    turn = both(wave(np.outer(kb, i), 13))
    cr, ci = wave(np.outer(i, k), 7)
    scale = 2.0 ** (-LOG_TOTAL / 2)
    last = np.block([[cr, ci], [-ci, cr]]) * scale
    return dict(
        mix=np_split(mix), owner=owner, low_in=low_in, low_out=low_out, steps=steps,
        inner=inner, turn=turn, last=np_split(last),
    )


def place():
    gx, gy, gz = (lax.axis_index(a) for a in AXES)
    return gz % 4, (gz // 4) % 4, (gz // 16) * 2 + gx, gy


def halves(x):
    high = x.astype(jnp.bfloat16)
    return high, (x - high.astype(jnp.float32)).astype(jnp.bfloat16)


def dot(a, b):
    return jnp.dot(a, b, preferred_element_type=jnp.float32)


def exchange_kernel(
    in_re, in_im, mix_hi, mix_lo, owner, low_in, low_out, steps, out,
    got, sent, back, done, w_hi, w_lo, own_t, in_t, out_t, step_t, in_fine, in_coarse, out_fine, out_coarse,
    send_sem, own_sem, table_sem, first_sem, second_sem, write_sem,
):
    x, y, z, core = place()
    me = (z % 2) * 64 + core * 32 + (z // 2) * 16 + y * 4 + x

    def partner(step):
        px = (x + step) % 4
        py = (y + step // 4) % 4
        pz = (z + step // 16) % 4
        pc = (core + step // 64) % 2
        gx, gz = pz % 2, (pz // 2) * 16 + py * 4 + px
        return gx * 64 + pc * 32 + gz, (gx, pc, gz)

    def push(src, dst, sem, device):
        pltpu.make_async_remote_copy(src, dst, send_sem, sem, device_id=device, device_id_type=MESH).start()

    def leg_one(i, _):
        chunk, step = i // 127, i % 127 + 1
        rows = pl.ds(chunk * ROWS, ROWS)
        d, device = partner(step)
        push(in_re.at[d, rows], got.at[rows, me], first_sem.at[chunk], device)
        push(in_im.at[d, rows], got.at[rows, N + me], first_sem.at[chunk], device)
        return 0

    own = [pltpu.make_async_copy(src.at[me], got.at[:, at + me], own_sem) for src, at in ((in_re, 0), (in_im, N))]
    loads = [
        pltpu.make_async_copy(src, dst, table_sem.at[n])
        for n, (src, dst) in enumerate(
            ((mix_hi, w_hi), (mix_lo, w_lo), (owner, own_t), (low_in, in_t), (low_out, out_t), (steps, step_t))
        )
    ]
    lax.fori_loop(0, 127 * CHUNKS, leg_one, 0)
    for copy in own + loads:
        copy.start()
    for copy in loads:
        copy.wait()

    def spread(column):
        return jnp.broadcast_to(column, (N, C))

    lane = lax.broadcasted_iota(jnp.int32, (N, C), 1)
    mine = [jnp.sum(jnp.where(lane == me, own_t[at : at + N], 0.0), axis=1, keepdims=True) for at in (0, N)]
    for low, fine, coarse, at, extra in ((in_t, in_fine, in_coarse, 0, mine), (out_t, out_fine, out_coarse, 32, None)):
        lr, li = low[:N], low[N:]
        if extra is not None:
            er, ei = spread(extra[0]), spread(extra[1])
            lr, li = lr * er - li * ei, lr * ei + li * er
        for e in range(8):
            sr, si = spread(step_t[:N, at + e : at + e + 1]), spread(step_t[N:, at + e : at + e + 1])
            fine[e, :N] = lr * sr - li * si
            fine[e, N:] = lr * si + li * sr
            coarse[e, :N] = spread(step_t[:N, at + 8 + e : at + 9 + e])
            coarse[e, N:] = spread(step_t[N:, at + 8 + e : at + 9 + e])

    def transform(src, dst, chunk, fine, coarse):
        def pair(q, _):
            b = chunk * ROWS + 2 * q
            hi, lo = halves(jnp.concatenate([src[b], src[b + 1]], axis=1))
            whi = w_hi[...]
            mixed = dot(whi, hi) + dot(whi, lo) + dot(w_lo[...], hi)
            for h in range(2):
                low, high = (b + h) % 8, (b + h) // 8
                fr, fi, cr, ci = fine[low, :N], fine[low, N:], coarse[high, :N], coarse[high, N:]
                tr, ti = fr * cr - fi * ci, fr * ci + fi * cr
                mr, mi = mixed[:N, h * C : (h + 1) * C], mixed[N:, h * C : (h + 1) * C]
                dst[b + h, :N] = mr * tr - mi * ti
                dst[b + h, N:] = mr * ti + mi * tr
            return 0

        lax.fori_loop(0, ROWS // 2, pair, 0)

    for copy in own:
        copy.wait()

    def there(chunk, _):
        rows = pl.ds(chunk * ROWS, ROWS)
        taken = got.at[rows, pl.ds(0, 254)]
        pltpu.make_async_copy(taken, taken, first_sem.at[chunk]).wait()
        transform(got, sent, chunk, in_fine, in_coarse)

        def leg_two(i, _):
            d, device = partner(i + 1)
            push(sent.at[rows, d], back.at[rows, me], second_sem.at[chunk], device)
            push(sent.at[rows, N + d], back.at[rows, N + me], second_sem.at[chunk], device)
            return 0

        lax.fori_loop(0, 127, leg_two, 0)
        for at in (0, N):
            back[rows, pl.ds(at + me, 1), :] = sent[rows, pl.ds(at + me, 1), :]
        return 0

    lax.fori_loop(0, CHUNKS, there, 0)

    def home(chunk, _):
        rows = pl.ds(chunk * ROWS, ROWS)
        taken = back.at[rows, pl.ds(0, 254)]
        pltpu.make_async_copy(taken, taken, second_sem.at[chunk]).wait()
        transform(back, done, chunk, out_fine, out_coarse)

        def write(r, _):
            b = chunk * ROWS + r
            pltpu.make_async_copy(done.at[b], out.at[:, b], write_sem).start()
            return 0

        lax.fori_loop(0, ROWS, write, 0)
        return 0

    lax.fori_loop(0, CHUNKS, home, 0)
    pltpu.make_async_copy(done, done, write_sem).wait()
    for _ in range(4):
        moved = got.at[:, pl.ds(0, 127)]
        pltpu.make_async_copy(moved, moved, send_sem).wait()


def finish_kernel(z, inner, turn, last_hi, last_lo, out_re, out_im, prob, hi_s, lo_s):
    count = z.shape[1]
    mat = inner[...]
    vr, vi = turn[:B], turn[B:]
    for q in range(count // 2):
        both = [jnp.concatenate([z[part, 2 * q], z[part, 2 * q + 1]], axis=1) for part in range(2)]
        hi, lo = halves(jnp.concatenate(both, axis=0))
        mixed = dot(mat, jnp.concatenate([hi, lo, hi], axis=0))
        for h in range(2):
            mr, mi = mixed[:B, h * C : (h + 1) * C], mixed[B:, h * C : (h + 1) * C]
            at = (2 * q + h) * B
            for value, lanes in ((mr * vr - mi * vi, slice(0, C)), (mr * vi + mi * vr, slice(C, 2 * C))):
                high, low = halves(value)
                hi_s[at : at + B, lanes] = high
                lo_s[at : at + B, lanes] = low
    result = dot(hi_s[...], last_hi[...]) + dot(lo_s[...], last_hi[...]) + dot(hi_s[...], last_lo[...])
    re = result[:, :C]
    im = result[:, C:]
    out_re[...] = re.reshape(out_re.shape)
    out_im[...] = im.reshape(out_im.shape)
    prob[...] = (re * re + im * im).reshape(prob.shape)


def solution(mesh):
    t = tables()
    f32, bf16 = jnp.float32, jnp.bfloat16
    anywhere = pl.BlockSpec(memory_space=pl.ANY)
    cube = pltpu.VMEM((B, 2 * N, C), f32)
    table = pltpu.VMEM((2 * N, C), f32)
    fan = pltpu.VMEM((8, 2 * N, C), f32)
    dma = pltpu.SemaphoreType.DMA

    exchange = pl.pallas_call(
        exchange_kernel,
        out_shape=jax.ShapeDtypeStruct((2 * N, B, C), f32),
        in_specs=[anywhere] * 8,
        out_specs=anywhere,
        scratch_shapes=[
            cube, cube, cube, cube,
            pltpu.VMEM((2 * N, 2 * N), bf16), pltpu.VMEM((2 * N, 2 * N), bf16),
            table, table, table, table, fan, fan, fan, fan,
            dma, dma, dma((6,)), dma((CHUNKS,)), dma((CHUNKS,)), dma,
        ],
        compiler_params=pltpu.CompilerParams(has_side_effects=True, vmem_limit_bytes=60 << 20),
    )
    block = 8
    whole = lambda shape: pl.BlockSpec(shape, lambda i: (0,) * len(shape))
    finish = pl.pallas_call(
        finish_kernel,
        grid=(N // block,),
        out_shape=[jax.ShapeDtypeStruct((N, B, C), f32)] * 3,
        in_specs=[
            pl.BlockSpec((2, block, B, C), lambda i: (0, i, 0, 0)),
            whole((2 * B, 6 * B)), whole((2 * B, C)), whole((2 * C, 2 * C)), whole((2 * C, 2 * C)),
        ],
        out_specs=[pl.BlockSpec((block, B, C), lambda i: (i, 0, 0))] * 3,
        scratch_shapes=[pltpu.VMEM((block * B, 2 * C), bf16)] * 2,
        compiler_params=pltpu.CompilerParams(dimension_semantics=("arbitrary",), vmem_limit_bytes=40 << 20),
    )

    def on_device(state_re, state_im):
        cut = (N, B, C)
        z = exchange(
            state_re.reshape(cut), state_im.reshape(cut), *map(jnp.asarray, t["mix"]),
            *(jnp.asarray(t[name]) for name in ("owner", "low_in", "low_out", "steps")),
        )
        outs = finish(z.reshape(2, N, B, C), jnp.asarray(t["inner"]), jnp.asarray(t["turn"]), *map(jnp.asarray, t["last"]))
        return tuple(o.reshape(N * B * C) for o in outs)

    spec = P(AXES)
    return jax.shard_map(on_device, mesh=mesh, in_specs=(spec, spec), out_specs=(spec,) * 3, check_vma=False)
```

profile of v0, /device:TPU:1, one launch (start us, length us, event | category | flops | bytes accessed | tf_op | source)
XLA Modules:
  0.0 218.0 jit_solution(231476935835606115)
XLA Ops:
  0.6 0.0 copy-start.1
  0.6 0.0 copy-start.2
  0.7 0.0 copy-start.3
  0.7 0.0 copy-start.4
  0.7 201.0 %shard_map.139 = f32[256,64,128]{2,1,0:T(8,128)} custom-call(f32[128,64,128]{2,1,0:T(8,128)} %bitcast.7, f32[128,64,128]{2,1,0:T(8,128)} %bitcast.8, bf16[256,256]{1,0:T(8,128)(2,1)} %constant.20.clone.mix_hi, bf16[256,256]{1,0:T(8,128)(2,1)} %constant.21.clone.mix_lo, f32[256,128]{1,0:T(8,128)} %constant.22.clone.owner, f32[256,128]{1,0:T(8,128)} %constant.23.clone.low_in, ...), custom_call_target="tpu_custom_call" | custom-call | tf_op jit(solution)/shard_map/pallas_call | solution.py:263
  201.7 0.0 copy-done.1
  201.7 0.0 copy-done.2
  201.7 0.0 copy-done.3
  201.8 0.0 copy-done.4
  201.8 0.0 copy-start
  201.8 3.4 %copy-done = f32[256,64,128]{2,1,0:T(8,128)S(1)} copy-done((f32[256,64,128]{2,1,0:T(8,128)S(1)}, f32[256,64,128]{2,1,0:T(8,128)}, u32[]{:S(2)}) %copy-start) | copy-done | bytes 8388632
  205.1 12.9 %shard_map.140 = (f32[128,64,128]{2,1,0:T(8,128)}, f32[128,64,128]{2,1,0:T(8,128)}, f32[128,64,128]{2,1,0:T(8,128)}) custom-call(f32[2,128,64,128]{3,2,1,0:T(8,128)S(1)} %bitcast.6, bf16[128,384]{1,0:T(8,128)(2,1)S(1)} %copy-done.3, f32[128,128]{1,0:T(8,128)S(1)} %copy-done.4, bf16[256,256]{1,0:T(8,128)(2,1)S(1)} %copy-done.2, bf16[256,256]{1,0:T(8,128)(2,1)S(1)} %copy-done.1), custom_call_target="tpu_custom_call" | custom-call | tf_op jit(solution)/shard_map/pallas_call | solution.py:267
Async XLA Ops:
  0.6 201.1 %copy-start.1 = (bf16[256,256]{1,0:T(8,128)(2,1)S(1)}, bf16[256,256]{1,0:T(8,128)(2,1)}, u32[]{:S(2)}) copy-start(bf16[256,256]{1,0:T(8,128)(2,1)} %constant.29.clone.last_lo) | copy-start | bytes 393220
  0.6 201.1 %copy-start.2 = (bf16[256,256]{1,0:T(8,128)(2,1)S(1)}, bf16[256,256]{1,0:T(8,128)(2,1)}, u32[]{:S(2)}) copy-start(bf16[256,256]{1,0:T(8,128)(2,1)} %constant.28.clone.last_hi) | copy-start | bytes 393220
  0.7 201.1 %copy-start.3 = (bf16[128,384]{1,0:T(8,128)(2,1)S(1)}, bf16[128,384]{1,0:T(8,128)(2,1)}, u32[]{:S(2)}) copy-start(bf16[128,384]{1,0:T(8,128)(2,1)} %constant.26.clone.inner) | copy-start | bytes 294916
  0.7 201.1 %copy-start.4 = (f32[128,128]{1,0:T(8,128)S(1)}, f32[128,128]{1,0:T(8,128)}, u32[]{:S(2)}) copy-start(f32[128,128]{1,0:T(8,128)} %constant.27.clone.turn) | copy-start | bytes 196612
  201.8 3.4 %copy-start = (f32[256,64,128]{2,1,0:T(8,128)S(1)}, f32[256,64,128]{2,1,0:T(8,128)}, u32[]{:S(2)}) copy-start(f32[256,64,128]{2,1,0:T(8,128)} %shard_map.139) | copy-start | bytes 25165828
where the time goes:
time: 219 us; the launch traced here: 218 us
  Pallas kernels  214 us (98%)
  local copies, waits for them, and re-layouts  3.4 us (2%)
    pallas_call x1, Pallas kernels, on_device(): exchange(state_re.reshape(cut), state_im.reshape(cut), *map(jnp.asarray,...  201 us
    pallas_call x1, Pallas kernels, on_device(): finish(z.reshape(2, N, B, C), jnp.asarray(t['inner']), jnp.asarray(t['tur...  12.9 us

commit v1 on v0

v1 whole, which is shorter than its diff:
```python
import functools

import jax
import jax.numpy as jnp
import numpy as np
from jax import lax
from jax.experimental import pallas as pl
from jax.experimental.pallas import tpu as pltpu
from jax.sharding import PartitionSpec as P

MESH = pl.DeviceIdType.MESH
AXES = ("gx", "gy", "gz")
N, B, C = 128, 64, 128
CHUNKS = 8
ROWS = B // CHUNKS
LOG_TOTAL = 27


def rev(values, bits):
    values = np.asarray(values)
    return sum(((values >> i) & 1) << (bits - 1 - i) for i in range(bits))


def wave(product, bits):
    angle = 2.0 * np.pi * (product % (1 << bits)) / (1 << bits)
    return np.cos(angle), np.sin(angle)


def np_split(matrix):
    high = np.asarray(matrix, np.float32).astype(jnp.bfloat16)
    low = (np.asarray(matrix, np.float64) - high.astype(np.float64)).astype(jnp.bfloat16)
    return high, low


def tables():
    i = np.arange(N)
    k = rev(i, 7)
    wr, wi = wave(np.outer(k, i), 7)
    mix = np.block([[wr, -wi], [wi, wr]])
    both = lambda pair: np.concatenate(pair, axis=0).astype(np.float32)
    owner = both(wave(np.outer(k, i), 14))
    low_in = both(wave(np.outer(k, i), 27))
    low_out = both(wave(np.outer(k, i), 20))
    e = np.arange(8)
    steps = np.zeros((2 * N, C), np.float32)
    for at, bits in ((0, 20), (32, 13)):
        steps[:, at : at + 8] = both(wave(np.outer(k, e), bits))
        steps[:, at + 8 : at + 16] = both(wave(np.outer(k, 8 * e), bits))
    j = np.arange(8)
    middle = [both(wave(np.outer(j, 128 * chunk + i), 13)) for chunk in range(CHUNKS)]
    turn = both(wave(np.outer(j, i), 10))
    cr, ci = wave(np.outer(i, k), 7)
    scale = 2.0 ** (-LOG_TOTAL / 2)
    last = np.block([[cr, ci], [-ci, cr]]) * scale
    return dict(
        mix=np_split(mix), owner=owner, low_in=low_in, low_out=low_out, steps=steps,
        middle=np.stack(middle), turn=turn, last=np_split(last),
    )


def place():
    gx, gy, gz = (lax.axis_index(a) for a in AXES)
    return gz % 4, (gz // 4) % 4, (gz // 16) * 2 + gx, gy


def halves(x):
    high = x.astype(jnp.bfloat16)
    return high, (x - high.astype(jnp.float32)).astype(jnp.bfloat16)


def dot(a, b):
    return jnp.dot(a, b, preferred_element_type=jnp.float32)


def eight(v):
    def add(p, q):
        return p[0] + q[0], p[1] + q[1]

    def sub(p, q):
        return p[0] - q[0], p[1] - q[1]

    def turn(p):
        return -p[1], p[0]

    def four(p):
        s, d, t, u = add(p[0], p[2]), sub(p[0], p[2]), add(p[1], p[3]), turn(sub(p[1], p[3]))
        return add(s, t), add(d, u), sub(s, t), sub(d, u)

    root = 0.5**0.5
    even, odd = four(v[0::2]), four(v[1::2])
    r, i = odd[1]
    one = ((r - i) * root, (r + i) * root)
    r, i = odd[3]
    three = ((r + i) * -root, (r - i) * root)
    odd = (odd[0], one, turn(odd[2]), three)
    return [add(even[k], odd[k]) for k in range(4)] + [sub(even[k], odd[k]) for k in range(4)]


def times(p, q):
    return p[0] * q[0] - p[1] * q[1], p[0] * q[1] + p[1] * q[0]


def exchange_kernel(
    in_re, in_im, mix_hi, mix_lo, owner, low_in, low_out, steps, middle, out,
    got, sent, back, work, w_hi, w_lo, own_t, in_t, out_t, step_t, middle_t, in_fine, in_coarse, out_fine, out_coarse,
    send_sem, own_sem, table_sem, first_sem, second_sem,
):
    x, y, z, core = place()
    me = (z % 2) * 64 + core * 32 + (z // 2) * 16 + y * 4 + x

    def partner(step):
        px = (x + step) % 4
        py = (y + step // 4) % 4
        pz = (z + step // 16) % 4
        pc = (core + step // 64) % 2
        gx, gz = pz % 2, (pz // 2) * 16 + py * 4 + px
        return gx * 64 + pc * 32 + gz, (gx, pc, gz)

    def push(src, dst, sem, device):
        pltpu.make_async_remote_copy(src, dst, send_sem, sem, device_id=device, device_id_type=MESH).start()

    def leg_one(i, _):
        chunk, step = i // 127, i % 127 + 1
        d, device = partner(step)
        push(in_re.at[d, :, chunk], got.at[chunk, :, me], first_sem.at[chunk], device)
        push(in_im.at[d, :, chunk], got.at[chunk, :, N + me], first_sem.at[chunk], device)
        return 0

    own = [
        pltpu.make_async_copy(src.at[me, :, chunk], got.at[chunk, :, at + me], own_sem)
        for src, at in ((in_re, 0), (in_im, N))
        for chunk in range(CHUNKS)
    ]
    loads = [
        pltpu.make_async_copy(src, dst, table_sem.at[n])
        for n, (src, dst) in enumerate(
            (
                (mix_hi, w_hi), (mix_lo, w_lo), (owner, own_t), (low_in, in_t), (low_out, out_t), (steps, step_t),
                (middle, middle_t),
            )
        )
    ]
    lax.fori_loop(0, 127 * CHUNKS, leg_one, 0)
    for copy in own + loads:
        copy.start()
    for copy in loads:
        copy.wait()

    def spread(column):
        return jnp.broadcast_to(column, (N, C))

    lane = lax.broadcasted_iota(jnp.int32, (N, C), 1)
    mine = [jnp.sum(jnp.where(lane == me, own_t[at : at + N], 0.0), axis=1, keepdims=True) for at in (0, N)]
    for low, fine, coarse, at, extra in ((in_t, in_fine, in_coarse, 0, mine), (out_t, out_fine, out_coarse, 32, None)):
        value = low[:N], low[N:]
        if extra is not None:
            value = times(value, (spread(extra[0]), spread(extra[1])))
        for e in range(8):
            step = spread(step_t[:N, at + e : at + e + 1]), spread(step_t[N:, at + e : at + e + 1])
            fine[e, :N], fine[e, N:] = times(value, step)
            coarse[e, :N] = spread(step_t[:N, at + 8 + e : at + 9 + e])
            coarse[e, N:] = spread(step_t[N:, at + 8 + e : at + 9 + e])

    def transform(src, dst, chunk, fine, coarse):
        def pair(q, _):
            hi, lo = halves(jnp.concatenate([src[2 * q], src[2 * q + 1]], axis=1))
            whi = w_hi[...]
            mixed = dot(whi, hi) + dot(whi, lo) + dot(w_lo[...], hi)
            for h in range(2):
                b = 2 * q + h
                turn = times((fine[chunk, :N], fine[chunk, N:]), (coarse[b, :N], coarse[b, N:]))
                part = mixed[:, h * C : (h + 1) * C]
                dst[b, :N], dst[b, N:] = times((part[:N], part[N:]), turn)
            return 0

        lax.fori_loop(0, ROWS // 2, pair, 0)

    for _ in range(2):
        pltpu.make_async_copy(in_re.at[0], in_re.at[0], own_sem).wait()

    def there(chunk, _):
        taken = got.at[chunk, :, pl.ds(0, 254)]
        pltpu.make_async_copy(taken, taken, first_sem.at[chunk]).wait()
        transform(got.at[chunk], sent.at[chunk], chunk, in_fine, in_coarse)

        def leg_two(i, _):
            d, device = partner(i + 1)
            push(sent.at[chunk, :, d], back.at[chunk, :, me], second_sem.at[chunk], device)
            push(sent.at[chunk, :, N + d], back.at[chunk, :, N + me], second_sem.at[chunk], device)
            return 0

        lax.fori_loop(0, 127, leg_two, 0)
        for at in (0, N):
            back[chunk, :, pl.ds(at + me, 1), :] = sent[chunk, :, pl.ds(at + me, 1), :]
        return 0

    lax.fori_loop(0, CHUNKS, there, 0)

    def home(chunk, _):
        taken = back.at[chunk, :, pl.ds(0, 254)]
        pltpu.make_async_copy(taken, taken, second_sem.at[chunk]).wait()
        transform(back.at[chunk], work, chunk, out_fine, out_coarse)

        def butterfly(r, _):
            re, im = pl.ds(pl.multiple_of(r * 8, 8), 8), pl.ds(pl.multiple_of(N + r * 8, 8), 8)
            for k, value in enumerate(eight([(work[b, re], work[b, im]) for b in range(8)])):
                turn = middle_t[chunk, k : k + 1], middle_t[chunk, 8 + k : 9 + k]
                out[chunk, k, re], out[chunk, k, im] = times(value, turn)
            return 0

        lax.fori_loop(0, N // 8, butterfly, 0)
        return 0

    lax.fori_loop(0, CHUNKS, home, 0)
    for _ in range(4):
        for chunk in range(CHUNKS):
            moved = got.at[chunk, :, pl.ds(0, 127)]
            pltpu.make_async_copy(moved, moved, send_sem).wait()


GROUP = 32


def finish_kernel(z, turn, last_hi, last_lo, out_re, out_im, prob, stage, out_sem):
    outs = (out_re, out_im, prob)

    def block(k, slot):
        @pl.when(k >= 2)
        def _():
            pltpu.make_async_copy(stage.at[slot], stage.at[slot], out_sem.at[slot]).wait()

        for g in range(N // GROUP):
            re, im = slice(g * GROUP, (g + 1) * GROUP), slice(N + g * GROUP, N + (g + 1) * GROUP)
            high, low = [], []
            for n, value in enumerate(eight([(z[b, k, re], z[b, k, im]) for b in range(8)])):
                parts = [halves(v) for v in times(value, (turn[n : n + 1], turn[8 + n : 9 + n]))]
                high.append(jnp.concatenate([p[0] for p in parts], axis=1))
                low.append(jnp.concatenate([p[1] for p in parts], axis=1))
            high, low = jnp.concatenate(high, axis=0), jnp.concatenate(low, axis=0)
            result = dot(high, last_hi[...]) + dot(low, last_hi[...]) + dot(high, last_lo[...])
            for n in range(8):
                r, i = result[n * GROUP : (n + 1) * GROUP, :C], result[n * GROUP : (n + 1) * GROUP, C:]
                for o, value in enumerate((r, i, r * r + i * i)):
                    stage[slot, o, n, re] = value
        first = (k % 2) * 32 + (k // 2 % 2) * 16 + (k // 4) * 8
        for o, ref in enumerate(outs):
            for n in range(8):
                pltpu.make_async_copy(stage.at[slot, o, n], ref.at[:, first + int(rev(n, 3))], out_sem.at[slot]).start()

    def two(i, _):
        for slot in range(2):
            block(2 * i + slot, slot)
        return 0

    lax.fori_loop(0, 4, two, 0)
    for slot in range(2):
        pltpu.make_async_copy(stage.at[slot], stage.at[slot], out_sem.at[slot]).wait()


def solution(mesh):
    t = tables()
    f32, bf16 = jnp.float32, jnp.bfloat16
    anywhere, near = pl.BlockSpec(memory_space=pl.ANY), pl.BlockSpec(memory_space=pltpu.VMEM)
    far = pl.BlockSpec(memory_space=pltpu.HBM)
    cube = pltpu.VMEM((CHUNKS, ROWS, 2 * N, C), f32)
    table = pltpu.VMEM((2 * N, C), f32)
    fan = pltpu.VMEM((8, 2 * N, C), f32)
    dma = pltpu.SemaphoreType.DMA

    exchange = pl.pallas_call(
        exchange_kernel,
        out_shape=cube,
        in_specs=[far] * 2 + [anywhere] * 7,
        out_specs=near,
        scratch_shapes=[
            cube, cube, cube, fan,
            pltpu.VMEM((2 * N, 2 * N), bf16), pltpu.VMEM((2 * N, 2 * N), bf16),
            table, table, table, table, pltpu.VMEM((CHUNKS, 16, C), f32), fan, fan, fan, fan,
            dma, dma, dma((7,)), dma((CHUNKS,)), dma((CHUNKS,)),
        ],
        compiler_params=pltpu.CompilerParams(has_side_effects=True, vmem_limit_bytes=48 << 20),
    )
    finish = pl.pallas_call(
        finish_kernel,
        out_shape=[jax.ShapeDtypeStruct((N, B, C), f32)] * 3,
        in_specs=[near] * 4,
        out_specs=[far] * 3,
        scratch_shapes=[pltpu.VMEM((2, 3, 8, N, C), f32), dma((2,))],
        compiler_params=pltpu.CompilerParams(vmem_limit_bytes=24 << 20),
    )

    def on_device(state_re, state_im):
        cut = (N, 8, 8, C)
        states = [pltpu.with_memory_space_constraint(s.reshape(cut), pltpu.HBM) for s in (state_re, state_im)]
        names = ("owner", "low_in", "low_out", "steps", "middle")
        z = exchange(*states, *map(jnp.asarray, t["mix"]), *(jnp.asarray(t[name]) for name in names))
        z = pltpu.with_memory_space_constraint(z, pltpu.VMEM)
        outs = finish(z, jnp.asarray(t["turn"]), *map(jnp.asarray, t["last"]))
        return tuple(o.reshape(N * B * C) for o in outs)

    spec = P(AXES)
    return jax.shard_map(on_device, mesh=mesh, in_specs=(spec, spec), out_specs=(spec,) * 3, check_vma=False)
```

time: 219 us -> 212 us (0.968)
  Pallas kernels: 214 us -> 209 us
  local copies, waits for them, and re-layouts: 3.4 us -> 0.02 us
    pallas_call x2, Pallas kernels: 214 us -> 209 us  [the longest x1 200 us: on_device(): exchange(*states, *map(jnp.asarray, t['mix']), *(jnp.asarray(t[name]) for...]
    unnamed x10 -> x6, local copies, waits for them, and re-layouts: 3.4 us -> 0.02 us
where the time goes in v1:
time: 212 us; the launch traced here: 209 us
  Pallas kernels  209 us (99%)
    pallas_call x1, Pallas kernels, on_device(): exchange(*states, *map(jnp.asarray, t['mix']), *(jnp.asarray(t[name]) for...  200 us
    pallas_call x1, Pallas kernels, on_device(): outs = finish(z, jnp.asarray(t['turn']), *map(jnp.asarray, t['last']))  8.13 us

profile of v1, /device:TPU:1, one launch (start us, length us, event | category | flops | bytes accessed | tf_op | source)
XLA Modules:
  0.0 209.3 jit_solution(7036726245679617993)
XLA Ops:
  0.6 0.0 copy-start
  0.6 0.0 copy-start.1
  0.7 0.0 copy-start.2
  0.7 200.4 %shard_map.139.z = f32[8,8,256,128]{3,2,1,0:T(8,128)S(1)} custom-call(f32[128,8,8,128]{3,2,1,0:T(8,128)} %bitcast.5, f32[128,8,8,128]{3,2,1,0:T(8,128)} %bitcast.6, bf16[256,256]{1,0:T(8,128)(2,1)} %constant.20.clone.mix_hi, bf16[256,256]{1,0:T(8,128)(2,1)} %constant.21.clone.mix_lo, f32[256,128]{1,0:T(8,128)} %constant.22.clone.owner, ...), custom_call_target="tpu_custom_call" | custom-call | tf_op jit(solution)/shard_map/pallas_call | solution.py:296
  201.1 0.0 copy-done
  201.1 0.0 copy-done.1
  201.1 0.0 copy-done.2
  201.1 8.1 %shard_map.140 = (f32[128,64,128]{2,1,0:T(8,128)}, f32[128,64,128]{2,1,0:T(8,128)}, f32[128,64,128]{2,1,0:T(8,128)}) custom-call(f32[8,8,256,128]{3,2,1,0:T(8,128)S(1)} %shard_map.139.z, f32[16,128]{1,0:T(8,128)S(1)} %copy-done.2, bf16[256,256]{1,0:T(8,128)(2,1)S(1)} %copy-done.1, bf16[256,256]{1,0:T(8,128)(2,1)S(1)} %copy-done), custom_call_target="tpu_custom_call" | custom-call | tf_op jit(solution)/shard_map/pallas_call | solution.py:298
Async XLA Ops:
  0.6 200.5 %copy-start = (bf16[256,256]{1,0:T(8,128)(2,1)S(1)}, bf16[256,256]{1,0:T(8,128)(2,1)}, u32[]{:S(2)}) copy-start(bf16[256,256]{1,0:T(8,128)(2,1)} %constant.29.clone.last_lo) | copy-start | bytes 393220
  0.6 200.5 %copy-start.1 = (bf16[256,256]{1,0:T(8,128)(2,1)S(1)}, bf16[256,256]{1,0:T(8,128)(2,1)}, u32[]{:S(2)}) copy-start(bf16[256,256]{1,0:T(8,128)(2,1)} %constant.28.clone.last_hi) | copy-start | bytes 393220
  0.7 200.5 %copy-start.2 = (f32[16,128]{1,0:T(8,128)S(1)}, f32[16,128]{1,0:T(8,128)}, u32[]{:S(2)}) copy-start(f32[16,128]{1,0:T(8,128)} %constant.27.clone.turn) | copy-start | bytes 24580

commit v2 on v1

--- a/solution.py
+++ b/solution.py
@@ -14,6 +14,7 @@
 CHUNKS = 8
 ROWS = B // CHUNKS
 LOG_TOTAL = 27
+LINES = (64, 2, 8, 32, 1, 4, 16, 3, 12, 48)
 
 
 def rev(values, bits):
@@ -102,8 +103,8 @@
 
 def exchange_kernel(
     in_re, in_im, mix_hi, mix_lo, owner, low_in, low_out, steps, middle, out,
-    got, sent, back, work, w_hi, w_lo, own_t, in_t, out_t, step_t, middle_t, in_fine, in_coarse, out_fine, out_coarse,
-    send_sem, own_sem, table_sem, first_sem, second_sem,
+    got, sent, back, work, turn_t, w_hi, w_lo, own_t, in_t, out_t, step_t, middle_t, in_fine, in_coarse, out_fine, out_coarse,
+    send_sem, own_sem, table_sem, first_sem, second_sem, enter_sem,
 ):
     x, y, z, core = place()
     me = (z % 2) * 64 + core * 32 + (z // 2) * 16 + y * 4 + x
@@ -119,12 +120,54 @@
     def push(src, dst, sem, device):
         pltpu.make_async_remote_copy(src, dst, send_sem, sem, device_id=device, device_id_type=MESH).start()
 
-    def leg_one(i, _):
-        chunk, step = i // 127, i % 127 + 1
+    def leg_one(chunk, step):
         d, device = partner(step)
         push(in_re.at[d, :, chunk], got.at[chunk, :, me], first_sem.at[chunk], device)
         push(in_im.at[d, :, chunk], got.at[chunk, :, N + me], first_sem.at[chunk], device)
+
+    def lines(chunks):
+        def one(chunk, _):
+            for step in LINES:
+                leg_one(chunk, step)
+            return 0
+
+        lax.fori_loop(*chunks, one, 0)
+
+    def rest(chunk, _):
+        def other_core(i, _):
+            leg_one(chunk, 65 + i)
+            return 0
+
+        def layers(i, _):
+            leg_one(chunk, (i // 15 + 1) * 16 + i % 15 + 1)
+            return 0
+
+        def plane(i, _):
+            leg_one(chunk, (i // 3 + 1) * 4 + i % 3 + 1)
+            return 0
+
+        lax.fori_loop(0, 63, other_core, 0)
+        lax.fori_loop(0, 45, layers, 0)
+        lax.fori_loop(0, 9, plane, 0)
         return 0
+
+    def greet(sem, steps):
+        for step in steps:
+            pl.semaphore_signal(sem, inc=1, device_id=partner(step)[1], device_id_type=MESH)
+
+    barrier = pltpu.get_barrier_semaphore()
+    greet(barrier, LINES)
+    pl.semaphore_wait(barrier, len(LINES))
+    greet(enter_sem.at[0], (1, 2, 3))
+    lines((0, 2))
+    pl.semaphore_wait(enter_sem.at[0], 3)
+    greet(enter_sem.at[1], (16, 32, 48))
+    lines((2, 4))
+    pl.semaphore_wait(enter_sem.at[1], 3)
+    greet(enter_sem.at[2], (64,))
+    lines((4, 8))
+    pl.semaphore_wait(enter_sem.at[2], 1)
+    lax.fori_loop(0, CHUNKS, rest, 0)
 
     own = [
         pltpu.make_async_copy(src.at[me, :, chunk], got.at[chunk, :, at + me], own_sem)
@@ -140,7 +183,6 @@
             )
         )
     ]
-    lax.fori_loop(0, 127 * CHUNKS, leg_one, 0)
     for copy in own + loads:
         copy.start()
     for copy in loads:
@@ -161,27 +203,30 @@
             coarse[e, :N] = spread(step_t[:N, at + 8 + e : at + 9 + e])
             coarse[e, N:] = spread(step_t[N:, at + 8 + e : at + 9 + e])
 
-    def transform(src, dst, chunk, fine, coarse):
-        def pair(q, _):
+    def prepare(chunk, fine, coarse):
+        def one(b, _):
+            turn_t[b, :N], turn_t[b, N:] = times((fine[chunk, :N], fine[chunk, N:]), (coarse[b, :N], coarse[b, N:]))
+            return 0
+
+        lax.fori_loop(0, ROWS, one, 0)
+
+    def transform(src, dst):
+        for q in range(ROWS // 2):
             hi, lo = halves(jnp.concatenate([src[2 * q], src[2 * q + 1]], axis=1))
-            whi = w_hi[...]
-            mixed = dot(whi, hi) + dot(whi, lo) + dot(w_lo[...], hi)
+            mixed = dot(w_hi[...], hi) + dot(w_hi[...], lo) + dot(w_lo[...], hi)
             for h in range(2):
                 b = 2 * q + h
-                turn = times((fine[chunk, :N], fine[chunk, N:]), (coarse[b, :N], coarse[b, N:]))
                 part = mixed[:, h * C : (h + 1) * C]
-                dst[b, :N], dst[b, N:] = times((part[:N], part[N:]), turn)
-            return 0
-
-        lax.fori_loop(0, ROWS // 2, pair, 0)
+                dst[b, :N], dst[b, N:] = times((part[:N], part[N:]), (turn_t[b, :N], turn_t[b, N:]))
 
     for _ in range(2):
         pltpu.make_async_copy(in_re.at[0], in_re.at[0], own_sem).wait()
 
     def there(chunk, _):
+        prepare(chunk, in_fine, in_coarse)
         taken = got.at[chunk, :, pl.ds(0, 254)]
         pltpu.make_async_copy(taken, taken, first_sem.at[chunk]).wait()
-        transform(got.at[chunk], sent.at[chunk], chunk, in_fine, in_coarse)
+        transform(got.at[chunk], sent.at[chunk])
 
         def leg_two(i, _):
             d, device = partner(i + 1)
@@ -197,9 +242,10 @@
     lax.fori_loop(0, CHUNKS, there, 0)
 
     def home(chunk, _):
+        prepare(chunk, out_fine, out_coarse)
         taken = back.at[chunk, :, pl.ds(0, 254)]
         pltpu.make_async_copy(taken, taken, second_sem.at[chunk]).wait()
-        transform(back.at[chunk], work, chunk, out_fine, out_coarse)
+        transform(back.at[chunk], work)
 
         def butterfly(r, _):
             re, im = pl.ds(pl.multiple_of(r * 8, 8), 8), pl.ds(pl.multiple_of(N + r * 8, 8), 8)
@@ -218,17 +264,13 @@
             pltpu.make_async_copy(moved, moved, send_sem).wait()
 
 
-GROUP = 32
+GROUP = 16
+SEND = 64
 
 
 def finish_kernel(z, turn, last_hi, last_lo, out_re, out_im, prob, stage, out_sem):
     outs = (out_re, out_im, prob)
-
-    def block(k, slot):
-        @pl.when(k >= 2)
-        def _():
-            pltpu.make_async_copy(stage.at[slot], stage.at[slot], out_sem.at[slot]).wait()
-
+    for k in range(8):
         for g in range(N // GROUP):
             re, im = slice(g * GROUP, (g + 1) * GROUP), slice(N + g * GROUP, N + (g + 1) * GROUP)
             high, low = [], []
@@ -241,20 +283,14 @@
             for n in range(8):
                 r, i = result[n * GROUP : (n + 1) * GROUP, :C], result[n * GROUP : (n + 1) * GROUP, C:]
                 for o, value in enumerate((r, i, r * r + i * i)):
-                    stage[slot, o, n, re] = value
-        first = (k % 2) * 32 + (k // 2 % 2) * 16 + (k // 4) * 8
-        for o, ref in enumerate(outs):
-            for n in range(8):
-                pltpu.make_async_copy(stage.at[slot, o, n], ref.at[:, first + int(rev(n, 3))], out_sem.at[slot]).start()
-
-    def two(i, _):
-        for slot in range(2):
-            block(2 * i + slot, slot)
-        return 0
-
-    lax.fori_loop(0, 4, two, 0)
-    for slot in range(2):
-        pltpu.make_async_copy(stage.at[slot], stage.at[slot], out_sem.at[slot]).wait()
+                    stage[k, o, n, re] = value
+            if (g + 1) * GROUP % SEND == 0:
+                rows = slice((g + 1) * GROUP - SEND, (g + 1) * GROUP)
+                for o, ref in enumerate(outs):
+                    for n in range(8):
+                        place_of = int(rev(k + 8 * n, 6))
+                        pltpu.make_async_copy(stage.at[k, o, n, rows], ref.at[rows, place_of], out_sem).start()
+    pltpu.make_async_copy(stage, stage, out_sem).wait()
 
 
 def solution(mesh):
@@ -273,20 +309,20 @@
         in_specs=[far] * 2 + [anywhere] * 7,
         out_specs=near,
         scratch_shapes=[
-            cube, cube, cube, fan,
+            cube, cube, cube, fan, fan,
             pltpu.VMEM((2 * N, 2 * N), bf16), pltpu.VMEM((2 * N, 2 * N), bf16),
             table, table, table, table, pltpu.VMEM((CHUNKS, 16, C), f32), fan, fan, fan, fan,
-            dma, dma, dma((7,)), dma((CHUNKS,)), dma((CHUNKS,)),
+            dma, dma, dma((7,)), dma((CHUNKS,)), dma((CHUNKS,)), pltpu.SemaphoreType.REGULAR((3,)),
         ],
-        compiler_params=pltpu.CompilerParams(has_side_effects=True, vmem_limit_bytes=48 << 20),
+        compiler_params=pltpu.CompilerParams(has_side_effects=True, collective_id=0, vmem_limit_bytes=48 << 20),
     )
     finish = pl.pallas_call(
         finish_kernel,
         out_shape=[jax.ShapeDtypeStruct((N, B, C), f32)] * 3,
         in_specs=[near] * 4,
         out_specs=[far] * 3,
-        scratch_shapes=[pltpu.VMEM((2, 3, 8, N, C), f32), dma((2,))],
-        compiler_params=pltpu.CompilerParams(vmem_limit_bytes=24 << 20),
+        scratch_shapes=[pltpu.VMEM((8, 3, 8, N, C), f32), dma],
+        compiler_params=pltpu.CompilerParams(vmem_limit_bytes=20 << 20),
     )
 
     def on_device(state_re, state_im):

time: 212 us -> 201 us (0.948); the launches traced: 209 us -> 200 us
  Pallas kernels: 209 us -> 200 us
    pallas_call x1, Pallas kernels: 200 us -> 195 us  [on_device(): exchange(*states, *map(jnp.asarray, t['mix']), *(jnp.asarray(t[name]) for...]
    pallas_call x1, Pallas kernels: 8.13 us -> 4.87 us  [on_device(): outs = finish(z, jnp.asarray(t['turn']), *map(jnp.asarray, t['last']))]
where the time goes in v2:
time: 201 us; the launch traced here: 200 us
  Pallas kernels  200 us (100%)
    pallas_call x1, Pallas kernels, on_device(): exchange(*states, *map(jnp.asarray, t['mix']), *(jnp.asarray(t[name]) for...  195 us
    pallas_call x1, Pallas kernels, on_device(): outs = finish(z, jnp.asarray(t['turn']), *map(jnp.asarray, t['last']))  4.87 us

profile of v2, /device:TPU:1, one launch (start us, length us, event | category | flops | bytes accessed | tf_op | source)
XLA Modules:
  0.0 200.4 jit_solution(12724919432052005790)
XLA Ops:
  0.6 0.0 copy-start
  0.6 0.0 copy-start.1
  0.7 0.0 copy-start.2
  0.7 194.9 %shard_map.139.z = f32[8,8,256,128]{3,2,1,0:T(8,128)S(1)} custom-call(f32[128,8,8,128]{3,2,1,0:T(8,128)} %bitcast.5, f32[128,8,8,128]{3,2,1,0:T(8,128)} %bitcast.6, bf16[256,256]{1,0:T(8,128)(2,1)} %constant.20.clone.mix_hi, bf16[256,256]{1,0:T(8,128)(2,1)} %constant.21.clone.mix_lo, f32[256,128]{1,0:T(8,128)} %constant.22.clone.owner, ...), custom_call_target="tpu_custom_call" | custom-call | tf_op jit(solution)/shard_map/pallas_call | solution.py:332
  195.5 0.0 copy-done
  195.5 0.0 copy-done.1
  195.6 0.0 copy-done.2
  195.6 4.9 %shard_map.140 = (f32[128,64,128]{2,1,0:T(8,128)}, f32[128,64,128]{2,1,0:T(8,128)}, f32[128,64,128]{2,1,0:T(8,128)}) custom-call(f32[8,8,256,128]{3,2,1,0:T(8,128)S(1)} %shard_map.139.z, f32[16,128]{1,0:T(8,128)S(1)} %copy-done.2, bf16[256,256]{1,0:T(8,128)(2,1)S(1)} %copy-done.1, bf16[256,256]{1,0:T(8,128)(2,1)S(1)} %copy-done), custom_call_target="tpu_custom_call" | custom-call | tf_op jit(solution)/shard_map/pallas_call | solution.py:334
Async XLA Ops:
  0.6 194.9 %copy-start = (bf16[256,256]{1,0:T(8,128)(2,1)S(1)}, bf16[256,256]{1,0:T(8,128)(2,1)}, u32[]{:S(2)}) copy-start(bf16[256,256]{1,0:T(8,128)(2,1)} %constant.29.clone.last_lo) | copy-start | bytes 393220
  0.6 194.9 %copy-start.1 = (bf16[256,256]{1,0:T(8,128)(2,1)S(1)}, bf16[256,256]{1,0:T(8,128)(2,1)}, u32[]{:S(2)}) copy-start(bf16[256,256]{1,0:T(8,128)(2,1)} %constant.28.clone.last_hi) | copy-start | bytes 393220
  0.7 194.9 %copy-start.2 = (f32[16,128]{1,0:T(8,128)S(1)}, f32[16,128]{1,0:T(8,128)}, u32[]{:S(2)}) copy-start(f32[16,128]{1,0:T(8,128)} %constant.27.clone.turn) | copy-start | bytes 24580

commit v3 on v2

--- a/solution.py
+++ b/solution.py
@@ -133,22 +133,36 @@
 
         lax.fori_loop(*chunks, one, 0)
 
+    def row(y_step, z_step, core_step):
+        py, pz, pc = (y + y_step) % 4, (z + z_step) % 4, (core + core_step) % 2
+        gx, gz = pz % 2, (pz // 2) * 16 + py * 4
+        return [(gx * 64 + pc * 32 + gz + px, (gx, pc, gz + px)) for px in xs]
+
+    xs = [(x + step) % 4 for step in range(4)]
+
+    def first_leg(chunk, targets):
+        for d, device in targets:
+            push(in_re.at[d, :, chunk], got.at[chunk, :, me], first_sem.at[chunk], device)
+            push(in_im.at[d, :, chunk], got.at[chunk, :, N + me], first_sem.at[chunk], device)
+
     def rest(chunk, _):
+        first_leg(chunk, row(0, 0, 1)[1:])
+
         def other_core(i, _):
-            leg_one(chunk, 65 + i)
+            first_leg(chunk, row(i % 4, i // 4, 1))
+            return 0
+
+        def planes(i, _):
+            first_leg(chunk, row((i + 1) * (1 - i // 3), (i - 2) * (i // 3), 0)[1:])
             return 0
 
         def layers(i, _):
-            leg_one(chunk, (i // 15 + 1) * 16 + i % 15 + 1)
-            return 0
-
-        def plane(i, _):
-            leg_one(chunk, (i // 3 + 1) * 4 + i % 3 + 1)
-            return 0
-
-        lax.fori_loop(0, 63, other_core, 0)
-        lax.fori_loop(0, 45, layers, 0)
-        lax.fori_loop(0, 9, plane, 0)
+            first_leg(chunk, row(i % 3 + 1, i // 3 + 1, 0))
+            return 0
+
+        lax.fori_loop(1, 16, other_core, 0)
+        lax.fori_loop(0, 6, planes, 0)
+        lax.fori_loop(0, 9, layers, 0)
         return 0
 
     def greet(sem, steps):
@@ -228,13 +242,35 @@
         pltpu.make_async_copy(taken, taken, first_sem.at[chunk]).wait()
         transform(got.at[chunk], sent.at[chunk])
 
-        def leg_two(i, _):
-            d, device = partner(i + 1)
-            push(sent.at[chunk, :, d], back.at[chunk, :, me], second_sem.at[chunk], device)
-            push(sent.at[chunk, :, N + d], back.at[chunk, :, N + me], second_sem.at[chunk], device)
-            return 0
-
-        lax.fori_loop(0, 127, leg_two, 0)
+        def second_leg(targets):
+            for d, device in targets:
+                push(sent.at[chunk, :, d], back.at[chunk, :, me], second_sem.at[chunk], device)
+                push(sent.at[chunk, :, N + d], back.at[chunk, :, N + me], second_sem.at[chunk], device)
+
+        def corners(i, _):
+            second_leg(row(i % 3 + 1, i // 3 % 3 + 1, i // 9)[1:])
+            return 0
+
+        def sides(i, _):
+            second_leg(row(i % 3 + 1, i // 3 % 3 + 1, i // 9)[:1])
+            return 0
+
+        def near_row(i):
+            return row((i % 6 + 1) * (1 - i % 6 // 3), (i % 6 - 2) * (i % 6 // 3), i // 6)
+
+        def planes(i, _):
+            second_leg(near_row(i)[1:])
+            return 0
+
+        def lines_last(i, _):
+            second_leg(near_row(i)[:1])
+            return 0
+
+        lax.fori_loop(0, 18, corners, 0)
+        lax.fori_loop(0, 12, planes, 0)
+        lax.fori_loop(0, 18, sides, 0)
+        lax.fori_loop(0, 12, lines_last, 0)
+        second_leg(row(0, 0, 0)[1:] + row(0, 0, 1)[1:] + row(0, 0, 1)[:1])
         for at in (0, N):
             back[chunk, :, pl.ds(at + me, 1), :] = sent[chunk, :, pl.ds(at + me, 1), :]
         return 0
@@ -248,20 +284,20 @@
         transform(back.at[chunk], work)
 
         def butterfly(r, _):
-            re, im = pl.ds(pl.multiple_of(r * 8, 8), 8), pl.ds(pl.multiple_of(N + r * 8, 8), 8)
-            for k, value in enumerate(eight([(work[b, re], work[b, im]) for b in range(8)])):
-                turn = middle_t[chunk, k : k + 1], middle_t[chunk, 8 + k : 9 + k]
-                out[chunk, k, re], out[chunk, k, im] = times(value, turn)
-            return 0
-
-        lax.fori_loop(0, N // 8, butterfly, 0)
+            for at in range(0, 32, 8):
+                re, im = pl.ds(pl.multiple_of(r * 32 + at, 8), 8), pl.ds(pl.multiple_of(N + r * 32 + at, 8), 8)
+                for k, value in enumerate(eight([(work[b, re], work[b, im]) for b in range(8)])):
+                    turn = middle_t[chunk, k : k + 1], middle_t[chunk, 8 + k : 9 + k]
+                    out[chunk, k, re], out[chunk, k, im] = times(value, turn)
+            return 0
+
+        lax.fori_loop(0, N // 32, butterfly, 0)
         return 0
 
     lax.fori_loop(0, CHUNKS, home, 0)
     for _ in range(4):
-        for chunk in range(CHUNKS):
-            moved = got.at[chunk, :, pl.ds(0, 127)]
-            pltpu.make_async_copy(moved, moved, send_sem).wait()
+        moved = got.at[:, :, pl.ds(0, 127)]
+        pltpu.make_async_copy(moved, moved, send_sem).wait()
 
 
 GROUP = 16

time: 201 us -> 201 us (level)
  no operation moved by 1% of the time
where the time goes in v3:
time: 201 us; the launch traced here: 200 us
  Pallas kernels  200 us (100%)
    pallas_call x1, Pallas kernels, on_device(): exchange(*states, *map(jnp.asarray, t['mix']), *(jnp.asarray(t[name]) for...  195 us
    pallas_call x1, Pallas kernels, on_device(): outs = finish(z, jnp.asarray(t['turn']), *map(jnp.asarray, t['last']))  4.87 us

profile of v3, /device:TPU:1, one launch (start us, length us, event | category | flops | bytes accessed | tf_op | source)
XLA Modules:
  0.0 200.4 jit_solution(8226496762291742037)
XLA Ops:
  0.6 0.0 copy-start
  0.6 0.0 copy-start.1
  0.7 0.0 copy-start.2
  0.7 194.8 %shard_map.139.z = f32[8,8,256,128]{3,2,1,0:T(8,128)S(1)} custom-call(f32[128,8,8,128]{3,2,1,0:T(8,128)} %bitcast.5, f32[128,8,8,128]{3,2,1,0:T(8,128)} %bitcast.6, bf16[256,256]{1,0:T(8,128)(2,1)} %constant.20.clone.mix_hi, bf16[256,256]{1,0:T(8,128)(2,1)} %constant.21.clone.mix_lo, f32[256,128]{1,0:T(8,128)} %constant.22.clone.owner, ...), custom_call_target="tpu_custom_call" | custom-call | tf_op jit(solution)/shard_map/pallas_call | solution.py:368
  195.5 0.0 copy-done
  195.5 0.0 copy-done.1
  195.5 0.0 copy-done.2
  195.5 4.9 %shard_map.140 = (f32[128,64,128]{2,1,0:T(8,128)}, f32[128,64,128]{2,1,0:T(8,128)}, f32[128,64,128]{2,1,0:T(8,128)}) custom-call(f32[8,8,256,128]{3,2,1,0:T(8,128)S(1)} %shard_map.139.z, f32[16,128]{1,0:T(8,128)S(1)} %copy-done.2, bf16[256,256]{1,0:T(8,128)(2,1)S(1)} %copy-done.1, bf16[256,256]{1,0:T(8,128)(2,1)S(1)} %copy-done), custom_call_target="tpu_custom_call" | custom-call | tf_op jit(solution)/shard_map/pallas_call | solution.py:370
Async XLA Ops:
  0.6 194.8 %copy-start = (bf16[256,256]{1,0:T(8,128)(2,1)S(1)}, bf16[256,256]{1,0:T(8,128)(2,1)}, u32[]{:S(2)}) copy-start(bf16[256,256]{1,0:T(8,128)(2,1)} %constant.29.clone.last_lo) | copy-start | bytes 393220
  0.6 194.8 %copy-start.1 = (bf16[256,256]{1,0:T(8,128)(2,1)S(1)}, bf16[256,256]{1,0:T(8,128)(2,1)}, u32[]{:S(2)}) copy-start(bf16[256,256]{1,0:T(8,128)(2,1)} %constant.28.clone.last_hi) | copy-start | bytes 393220
  0.7 194.8 %copy-start.2 = (f32[16,128]{1,0:T(8,128)S(1)}, f32[16,128]{1,0:T(8,128)}, u32[]{:S(2)}) copy-start(f32[16,128]{1,0:T(8,128)} %constant.27.clone.turn) | copy-start | bytes 24580
